TPU v7x, 32 devices: a whole 2x2x4 slice. The times are simulated.
32 devices in a mesh: role: 4 (over z), dp: 2 (over x), tp: 4 (over y, core).
Axes of the slice: x: 2, y: 2, z: 4, core: 2. Of those that a mesh axis runs over, the one named last changes fastest.
Arguments:
- activations: bfloat16 [2048, 8192], P(('role', 'dp'), 'tp'), may hold values from -6 to 6
- cotangent: bfloat16 [2048, 14336], P(('role', 'dp'), 'tp'), may hold values from -6 to 6
- block_keep: int32 [8], P(('role', 'dp')), may hold values 0 or 1
- input_factor: float32 [64, 8192], P(('role', 'dp'), 'tp'), may hold values from -0.5 to 0.5
- input_mean: float32 [64, 8192], P(('role', 'dp'), 'tp'), may hold values from -6 to 6
- input_square: float32 [64, 8192], P(('role', 'dp'), 'tp'), may hold values from 0.5 to 4
- output_factor: float32 [64, 14336], P(('role', 'dp'), 'tp'), may hold values from -0.3125 to 0.3125
- output_mean: float32 [64, 14336], P(('role', 'dp'), 'tp'), may hold values from -6 to 6
- output_square: float32 [64, 14336], P(('role', 'dp'), 'tp'), may hold values from 0.5 to 4
- frozen_base_rows: bfloat16 [14336, 8192], P(('dp', 'tp')), may hold values from -0.0625 to 0.0625
- prompts: bfloat16 [1024, 8192], P(('role', 'dp', 'tp')), may hold values from -6 to 6
Outputs:
- updated_input: float32 [64, 8192], P(('role', 'dp'), 'tp')
- updated_output: float32 [64, 14336], P(('role', 'dp'), 'tp')
- mean_input: float32 [64, 8192], P(('role', 'dp'), 'tp')
- mean_output: float32 [64, 14336], P(('role', 'dp'), 'tp')
- square_input: float32 [64, 8192], P(('role', 'dp'), 'tp')
- square_output: float32 [64, 14336], P(('role', 'dp'), 'tp')
- merged_weight_rows: bfloat16 [14336, 8192], P(('dp', 'tp'))
- projected: bfloat16 [14336, 1024], P(('dp', 'tp'), 'role')
All inputs are finite; a program needn't handle non-finite values. No bound on the sum of `block_keep` on one device may be relied on, other than what follows from the above.
Results may differ from a plain program's by a relative error of at most 0.006.
Values may be sent and summed in bfloat16 or wider, within the bound.
A program may use at most 128 MiB of HBM per device.

v0:
```python
import jax
import jax.numpy as jnp
from jax import lax
from jax.sharding import PartitionSpec as P

ROLLOUT_TOKENS = 256


adapter_scale = 2.0
learn_rate = 0.004
beta_one = 0.9
beta_two = 0.95
epsilon = 1e-08
first_fix = 1.0 - 0.9**20
second_fix = 1.0 - 0.95**20


def adam_update(factor, moment, square, gradient):
    moment_new = beta_one * moment + (1.0 - beta_one) * gradient
    square_new = beta_two * square + (1.0 - beta_two) * gradient * gradient
    factor_new = factor - learn_rate * (moment_new / first_fix) / (
        jnp.sqrt(square_new / second_fix) + epsilon
    )
    return (factor_new, moment_new, square_new)


def masked(values, block_keep):
    blocks = block_keep.shape[0]
    reshaped_rows = values.reshape(blocks, values.shape[0] // blocks, values.shape[1])
    weighted = reshaped_rows * block_keep.astype(jnp.float32)[:, None, None]
    return weighted.reshape(values.shape).astype(jnp.bfloat16)


def contract_rows(left, right):
    return lax.dot_general(
        left, right, (((0,), (0,)), ((), ())), preferred_element_type=jnp.float32
    )


def contract_cols(left, right):
    return lax.dot_general(
        left, right, (((1,), (1,)), ((), ())), preferred_element_type=jnp.float32
    )


def body(
    activations,
    cotangent,
    block_keep,
    input_factor,
    input_mean,
    input_square,
    output_factor,
    output_mean,
    output_square,
    frozen_base_rows,
    prompts,
):
    input_rows, output_rows = (
        lax.all_gather(input_factor.astype(jnp.bfloat16), ("role", "dp"), axis=0, tiled=True),
        lax.all_gather(output_factor.astype(jnp.bfloat16), ("role", "dp"), axis=0, tiled=True),
    )
    low_input = jnp.dot(activations, input_rows.T, preferred_element_type=jnp.float32)
    low_grad = jnp.dot(cotangent, output_rows.T, preferred_element_type=jnp.float32)
    low_input, low_grad = lax.psum((low_input, low_grad), "tp")
    input_kept = masked(low_input, block_keep)
    grad_kept = masked(low_grad, block_keep)
    input_part = contract_rows(grad_kept, activations)
    output_part = contract_rows(input_kept, cotangent)
    group_input, group_output = (
        lax.psum_scatter(input_part, "role", scatter_dimension=0, tiled=True),
        lax.psum_scatter(output_part, "role", scatter_dimension=0, tiled=True),
    )
    input_sum, output_sum = (
        lax.psum_scatter(group_input, "dp", scatter_dimension=0, tiled=True),
        lax.psum_scatter(group_output, "dp", scatter_dimension=0, tiled=True),
    )
    adapter_factor_scale = adapter_scale / ROLLOUT_TOKENS
    input_new, input_moment, input_second = adam_update(
        input_factor, input_mean, input_square, input_sum * adapter_factor_scale
    )
    output_new, output_moment, output_second = adam_update(
        output_factor, output_mean, output_square, output_sum * adapter_factor_scale
    )
    input_send = input_new.astype(jnp.bfloat16)
    output_send = output_new.astype(jnp.bfloat16)
    input_cols, output_cols = (
        lax.all_gather(input_send, ("role", "dp"), axis=0, tiled=True),
        lax.all_gather(output_send, ("role", "dp"), axis=0, tiled=True),
    )
    input_whole, output_whole = (
        lax.all_gather(input_cols, "tp", axis=1, tiled=True),
        lax.all_gather(output_cols, "tp", axis=1, tiled=True),
    )
    rows_here = frozen_base_rows.shape[0]
    row_block = lax.axis_index("dp") * lax.axis_size("tp") + lax.axis_index("tp")
    output_slice = lax.dynamic_slice_in_dim(output_whole, row_block * rows_here, rows_here, 1)
    adapter_delta_rows = contract_rows(output_slice, input_whole)
    merged_weight_rows = (
        frozen_base_rows.astype(jnp.float32) + adapter_scale * adapter_delta_rows
    ).astype(jnp.bfloat16)
    group_prompts = lax.all_gather(prompts, ("dp", "tp"), axis=0, tiled=True)
    projected = contract_cols(merged_weight_rows, group_prompts)
    return (
        input_new,
        output_new,
        input_moment,
        output_moment,
        input_second,
        output_second,
        merged_weight_rows,
        projected.astype(jnp.bfloat16),
    )


def solution(mesh):
    placed = (
        P(("role", "dp"), "tp"),
        P(("role", "dp"), "tp"),
        P(("role", "dp")),
        P(("role", "dp"), "tp"),
        P(("role", "dp"), "tp"),
        P(("role", "dp"), "tp"),
        P(("role", "dp"), "tp"),
        P(("role", "dp"), "tp"),
        P(("role", "dp"), "tp"),
        P(("dp", "tp"), None),
        P(("role", "dp", "tp"), None),
    )
    return jax.shard_map(
        body,
        mesh=mesh,
        in_specs=placed,
        out_specs=(
            P(("role", "dp"), "tp"),
            P(("role", "dp"), "tp"),
            P(("role", "dp"), "tp"),
            P(("role", "dp"), "tp"),
            P(("role", "dp"), "tp"),
            P(("role", "dp"), "tp"),
            P(("dp", "tp"), None),
            P(("dp", "tp"), "role"),
        ),
        check_vma=False,
    )
```

profile of v0, /device:TPU:0, one launch (start us, length us, event | category | flops | bytes accessed | tf_op | source)
XLA Modules:
  0.0 323.7 jit_solution(6785489352362475291)
XLA Ops:
  7.2 0.0 copy-start
  7.2 0.0 copy-start.2
  7.2 0.0 all-reduce.3.cloned.1.call-start
  7.2 1.1 convert_element_type.31
  8.3 32.9 %all_gather.21 = bf16[64,3584]{1,0:T(8,128)(2,1)S(1)} all-gather(bf16[8,3584]{1,0:T(8,128)(2,1)S(1)} %convert_element_type.31), channel_id=1, replica_groups=mesh['role'=4,'dp'=2,'tp'=4] {'role','dp'}, dimensions={0}, use_global_device_ids=true | all-gather | bytes 516096 | tf_op jit(solution)/shard_map/all_gather | solution.py:61
  41.2 0.8 convert_element_type.34
  42.0 30.7 %all_gather.22 = bf16[64,2048]{1,0:T(8,128)(2,1)S(1)} all-gather(bf16[8,2048]{1,0:T(8,128)(2,1)S(1)} %convert_element_type.34), channel_id=1, replica_groups=mesh['role'=4,'dp'=2,'tp'=4] {'role','dp'}, dimensions={0}, use_global_device_ids=true | all-gather | bytes 294912 | tf_op jit(solution)/shard_map/all_gather | solution.py:60
  72.7 0.0 copy-done
  72.7 1.3 fusion.8
  74.0 2.3 fusion.9
  76.4 0.0 all-reduce.3.cloned.1.call-update
  76.4 0.0 reduce-scatter.5.cloned.1.call-start
  77.2 32.8 %all-reduce.3.cloned.1.call-done = (f32[256,64]{1,0:T(8,128)}, f32[256,64]{1,0:T(8,128)}) async-done(((f32[256,64]{1,0:T(8,128)}, f32[256,64]{1,0:T(8,128)}), (f32[256,64]{1,0:T(8,128)}, f32[256,64]{1,0:T(8,128)})) %all-reduce.3.cloned.1.call-update) | async-done | bytes 131088 | tf_op jit(solution)/shard_map/psum | solution.py:65
  110.0 0.0 copy-done.2
  110.0 2.0 fusion.1
  112.0 0.0 reduce-scatter.5.cloned.1.call-update
  112.0 0.0 reduce-scatter.9.cloned.1.call-start
  112.1 2.3 fusion.2
  114.4 0.0 reduce-scatter.9.cloned.1.call-update
  114.4 0.0 reduce-scatter.7.cloned.1.call-start
  114.4 20.2 %reduce-scatter.5.cloned.1.call-done = f32[16,2048]{1,0:T(8,128)} async-done(((f32[64,2048]{1,0:T(8,128)}), f32[16,2048]{1,0:T(8,128)}) %reduce-scatter.5.cloned.1.call-update) | async-done | bytes 131088 | tf_op jit(solution)/shard_map/reduce_scatter | solution.py:71
  134.7 0.0 reduce-scatter.7.cloned.1.call-update
  134.7 0.0 reduce-scatter.11.cloned.1.call-start
  134.7 26.3 %reduce-scatter.9.cloned.1.call-done = f32[16,3584]{1,0:T(8,128)} async-done(((f32[64,3584]{1,0:T(8,128)}), f32[16,3584]{1,0:T(8,128)}) %reduce-scatter.9.cloned.1.call-update) | async-done | bytes 229392 | tf_op jit(solution)/shard_map/reduce_scatter | solution.py:72
  161.0 0.0 reduce-scatter.11.cloned.1.call-update
  161.1 0.0 all-gather.6.cloned.1.call-start
  161.1 11.3 %reduce-scatter.7.cloned.1.call-done = f32[8,2048]{1,0:T(8,128)} async-done(((f32[16,2048]{1,0:T(8,128)}), f32[8,2048]{1,0:T(8,128)}) %reduce-scatter.7.cloned.1.call-update) | async-done | bytes 65552 | tf_op jit(solution)/shard_map/reduce_scatter | solution.py:75
  172.4 0.0 copy-done.4
  172.4 0.0 copy-done.7
  172.4 0.0 copy-done.8
  172.4 1.5 fusion.7
  173.9 32.9 %all_gather.25 = bf16[64,2048]{1,0:T(8,128)(2,1)} all-gather(bf16[8,2048]{1,0:T(8,128)(2,1)S(1)} %get-tuple-element.14), channel_id=1, replica_groups=mesh['role'=4,'dp'=2,'tp'=4] {'role','dp'}, dimensions={0}, use_global_device_ids=true | all-gather | bytes 294912 | tf_op jit(solution)/shard_map/all_gather | solution.py:88
  206.8 0.0 all-gather.6.cloned.1.call-update
  206.8 0.0 all-gather.4.cloned.1.call-start
  206.9 0.0 reduce-scatter.11.cloned.1.call-done
  206.9 0.0 copy-done.3
  206.9 0.0 copy-done.5
  206.9 0.0 copy-done.6
  206.9 1.7 fusion.6
  208.6 33.1 %all_gather.23 = bf16[64,3584]{1,0:T(8,128)(2,1)} all-gather(bf16[8,3584]{1,0:T(8,128)(2,1)S(1)} %get-tuple-element.10), channel_id=1, replica_groups=mesh['role'=4,'dp'=2,'tp'=4] {'role','dp'}, dimensions={0}, use_global_device_ids=true | all-gather | bytes 516096 | tf_op jit(solution)/shard_map/all_gather | solution.py:89
  241.7 0.0 all-gather.4.cloned.1.call-update
  241.7 0.0 all-gather.8.cloned.1.call-start
  241.7 0.7 all-gather.8.cloned.1.call-update
  242.5 0.0 all-gather.6.cloned.1.call-done
  242.5 20.4 %all-gather.4.cloned.1.call-done = bf16[64,14336]{1,0:T(8,128)(2,1)} async-done(((bf16[64,3584]{1,0:T(8,128)(2,1)}), bf16[64,14336]{1,0:T(8,128)(2,1)}) %all-gather.4.cloned.1.call-update) | async-done | bytes 1835024 | tf_op jit(solution)/shard_map/all_gather | solution.py:93
  262.9 23.8 %add_convert_fusion = bf16[1792,8192]{1,0:T(8,128)(2,1)} fusion(bf16[1792,8192]{1,0:T(8,128)(2,1)} %param.20, bf16[64,8192]{1,0:T(8,128)(2,1)} %all-gather.6.cloned.1.call-done, bf16[64,14336]{1,0:T(8,128)(2,1)} %all-gather.4.cloned.1.call-done, s32[]{:T(128)S(6)} %select_n.3), kind=kOutput, calls=%fused_computation | convolution fusion | flops 1937768448 | bytes 59998212 | tf_op jit(solution)/shard_map/dot_general | solution.py:35
  286.7 14.7 %all-gather.8.cloned.1.call-done = bf16[256,8192]{1,0:T(8,128)(2,1)} async-done(((bf16[32,8192]{1,0:T(8,128)(2,1)}), bf16[256,8192]{1,0:T(8,128)(2,1)}) %all-gather.8.cloned.1.call-update) | async-done | bytes 4194320 | tf_op jit(solution)/shard_map/all_gather | solution.py:102
  301.4 15.4 %convolution_convert_fusion = bf16[1792,256]{1,0:T(8,128)(2,1)} fusion(bf16[1792,8192]{1,0:T(8,128)(2,1)} %add_convert_fusion, bf16[256,8192]{1,0:T(8,128)(2,1)} %all-gather.8.cloned.1.call-done), kind=kOutput, calls=%fused_computation.1 | convolution fusion | flops 7516651520 | bytes 34471936 | tf_op jit(solution)/shard_map/dot_general | solution.py:41
  (8 shorter events, 0.0 us)
Async XLA Ops:
  7.2 65.6 %copy-start = (bf16[256,3584]{1,0:T(8,128)(2,1)S(1)}, bf16[256,3584]{1,0:T(8,128)(2,1)}, u32[]{:S(2)}) copy-start(bf16[256,3584]{1,0:T(8,128)(2,1)} %param.12) | copy-start | bytes 5505028
  7.2 102.8 %copy-start.2 = (bf16[256,2048]{1,0:T(8,128)(2,1)S(1)}, bf16[256,2048]{1,0:T(8,128)(2,1)}, u32[]{:S(2)}) copy-start(bf16[256,2048]{1,0:T(8,128)(2,1)} %param.11) | copy-start | bytes 3145732
  7.2 102.8 %all-reduce.3.cloned.1.call-start = ((), (), s32[]{:S(2)}) async-start(), calls=%async_computation.11 | async-start | bytes 524288 | tf_op jit(solution)/shard_map/psum | solution.py:65
  74.0 98.4 %copy-start.4 = (f32[8,2048]{1,0:T(8,128)S(1)}, f32[8,2048]{1,0:T(8,128)}, u32[]{:S(2)}) copy-start(f32[8,2048]{1,0:T(8,128)} %param.14) | copy-start | bytes 196612
  74.0 98.4 %copy-start.7 = (f32[8,2048]{1,0:T(8,128)S(1)}, f32[8,2048]{1,0:T(8,128)}, u32[]{:S(2)}) copy-start(f32[8,2048]{1,0:T(8,128)} %param.15) | copy-start | bytes 196612
  74.0 98.4 %copy-start.8 = (f32[8,2048]{1,0:T(8,128)S(1)}, f32[8,2048]{1,0:T(8,128)}, u32[]{:S(2)}) copy-start(f32[8,2048]{1,0:T(8,128)} %param.16) | copy-start | bytes 196612
  76.4 130.6 %copy-start.3 = (f32[8,3584]{1,0:T(8,128)S(1)}, f32[8,3584]{1,0:T(8,128)}, u32[]{:S(2)}) copy-start(f32[8,3584]{1,0:T(8,128)} %param.17) | copy-start | bytes 344068
  76.4 130.6 %copy-start.5 = (f32[8,3584]{1,0:T(8,128)S(1)}, f32[8,3584]{1,0:T(8,128)}, u32[]{:S(2)}) copy-start(f32[8,3584]{1,0:T(8,128)} %param.18) | copy-start | bytes 344068
  76.4 130.6 %copy-start.6 = (f32[8,3584]{1,0:T(8,128)S(1)}, f32[8,3584]{1,0:T(8,128)}, u32[]{:S(2)}) copy-start(f32[8,3584]{1,0:T(8,128)} %param.19) | copy-start | bytes 344068
  76.4 58.3 %reduce-scatter.5.cloned.1.call-start = ((), (), s32[]{:S(2)}) async-start(), calls=%async_computation.4 | async-start | bytes 655360 | tf_op jit(solution)/shard_map/reduce_scatter | solution.py:71
  112.0 49.0 %reduce-scatter.9.cloned.1.call-start = ((), (), s32[]{:S(2)}) async-start(), calls=%async_computation.6 | async-start | bytes 1146880 | tf_op jit(solution)/shard_map/reduce_scatter | solution.py:72
  114.4 58.0 %reduce-scatter.7.cloned.1.call-start = ((), (), s32[]{:S(2)}) async-start(), calls=%async_computation.5 | async-start | bytes 196608 | tf_op jit(solution)/shard_map/reduce_scatter | solution.py:75
  134.7 72.2 %reduce-scatter.11.cloned.1.call-start = ((), (), s32[]{:S(2)}) async-start(), calls=%async_computation.7 | async-start | bytes 344064 | tf_op jit(solution)/shard_map/reduce_scatter | solution.py:76
  161.1 81.4 %all-gather.6.cloned.1.call-start = ((), (), s32[]{:S(2)}) async-start(), calls=%async_computation.9 | async-start | bytes 1310720 | tf_op jit(solution)/shard_map/all_gather | solution.py:92
  206.8 56.1 %all-gather.4.cloned.1.call-start = ((), (), s32[]{:S(2)}) async-start(), calls=%async_computation.8 | async-start | bytes 2293760 | tf_op jit(solution)/shard_map/all_gather | solution.py:93
  241.7 59.7 %all-gather.8.cloned.1.call-start = ((), (), s32[]{:S(2)}) async-start(), calls=%async_computation.10 | async-start | bytes 4718592 | tf_op jit(solution)/shard_map/all_gather | solution.py:102
  301.4 15.4 %copy-start.1 = (bf16[256,3584]{1,0:T(8,128)(2,1)S(1)}, bf16[256,3584]{1,0:T(8,128)(2,1)}, u32[]{:S(2)}) copy-start(bf16[256,3584]{1,0:T(8,128)(2,1)} %param.12) | copy-start | bytes 5505028
Sparse Core Ops, SparseCore 0:
  76.5 33.4 all-reduce.2
  112.8 21.8 reduce-scatter.4
  137.6 23.4 reduce-scatter.8
  163.1 9.2 reduce-scatter.6
  174.5 11.9 reduce-scatter.10
  207.0 16.5 all-gather.5
  241.8 21.0 all-gather.3
  264.8 36.5 all-gather.7
where the time goes:
time: 324 us
  blocking collectives  130 us (40%)
  waiting for transfers between devices  127 us (39%)
  matrix products  47.2 us (15%)
  between operations  14.9 us (5%)
  other arithmetic  5.1 us (2%)
    all_gather x1, blocking collectives, body(): lax.all_gather(output_send, ('role', 'dp'), axis=0, tiled=True)  33.1 us
    all_gather x1, blocking collectives, body(): lax.all_gather(input_send, ('role', 'dp'), axis=0, tiled=True)  32.9 us
    all_gather x1, blocking collectives, body(): lax.all_gather(output_factor.astype(jnp.bfloat16), ('role', 'dp'), axis=0...  32.9 us
    psum x1, waiting for transfers between devices, body(): low_input, low_grad = lax.psum((low_input, low_grad), 'tp')  32.8 us
    all_gather x1, blocking collectives, body(): lax.all_gather(input_factor.astype(jnp.bfloat16), ('role', 'dp'), axis=0,...  30.7 us
    dot_general x3, matrix products, contract_rows(): lax.dot_general(left, right, (((0,), (0,)), ((), ())), preferred_element_...  28.1 us
    reduce_scatter x1, waiting for transfers between devices, body(): lax.psum_scatter(output_part, 'role', scatter_dimension=0, tiled=True)  26.3 us
    all_gather x1, waiting for transfers between devices, body(): lax.all_gather(output_cols, 'tp', axis=1, tiled=True)  20.4 us
  transfers between devices with their start and end apart: 8, of which 6 were waited for; matrix products, arithmetic and copies ran while one was open for 9% of the time, Pallas kernels for 0%

commit v1 on v0

v1 whole, which is shorter than its diff:
```python
import functools

import jax
import jax.numpy as jnp
from jax import lax
from jax.experimental import pallas as pl
from jax.experimental.pallas import tpu as pltpu
from jax.sharding import PartitionSpec as P

ROLLOUT_TOKENS = 256


adapter_scale = 2.0
learn_rate = 0.004
beta_one = 0.9
beta_two = 0.95
epsilon = 1e-08
first_fix = 1.0 - 0.9**20
second_fix = 1.0 - 0.95**20


def adam_update(factor, moment, square, gradient):
    moment_new = beta_one * moment + (1.0 - beta_one) * gradient
    square_new = beta_two * square + (1.0 - beta_two) * gradient * gradient
    factor_new = factor - learn_rate * (moment_new / first_fix) / (
        jnp.sqrt(square_new / second_fix) + epsilon
    )
    return (factor_new, moment_new, square_new)


def masked(values, block_keep):
    blocks = block_keep.shape[0]
    reshaped_rows = values.reshape(blocks, values.shape[0] // blocks, values.shape[1])
    weighted = reshaped_rows * block_keep.astype(jnp.float32)[:, None, None]
    return weighted.reshape(values.shape).astype(jnp.bfloat16)


def contract_rows(left, right):
    return lax.dot_general(
        left, right, (((0,), (0,)), ((), ())), preferred_element_type=jnp.float32
    )


def contract_cols(left, right):
    return lax.dot_general(
        left, right, (((1,), (1,)), ((), ())), preferred_element_type=jnp.float32
    )


VMEM = pl.BlockSpec(memory_space=pltpu.VMEM)
MESH = pl.DeviceIdType.MESH


def places():
    return tuple(lax.axis_index(name) for name in ("role", "dp", "tp"))


def sizes():
    return tuple(lax.axis_size(name) for name in ("role", "dp", "tp"))


def enter(peers):
    barrier = pltpu.get_barrier_semaphore()
    for peer in peers:
        pl.semaphore_signal(barrier, inc=1, device_id=peer, device_id_type=MESH)
    pl.semaphore_wait(barrier, len(peers))


def send(source, target, send_sem, recv_sem, peer):
    copy = pltpu.make_async_remote_copy(
        src_ref=source,
        dst_ref=target,
        send_sem=send_sem,
        recv_sem=recv_sem,
        device_id=peer,
        device_id_type=MESH,
    )
    copy.start()
    return copy


def landed(slot, sem):
    pltpu.make_async_copy(slot, slot, sem).wait()


def communicate(kernel, name, outs, scratch, collective_id, args):
    return pl.pallas_call(
        kernel,
        name=name,
        out_shape=outs,
        in_specs=[VMEM] * len(args),
        out_specs=[VMEM] * len(outs),
        scratch_shapes=scratch,
        compiler_params=pltpu.CompilerParams(
            collective_id=collective_id,
            has_side_effects=True,
            vmem_limit_bytes=40 * 1024 * 1024,
        ),
        cost_estimate=pl.CostEstimate(
            flops=10**9, bytes_accessed=10**7, transcendentals=0
        ),
    )(*args)


def dma(*shape):
    return pltpu.SemaphoreType.DMA(shape)


def gather_kernel(count, *refs):
    ins, outs = refs[:count], refs[count : 2 * count]
    own, send_role, recv_role, send_dp, recv_dp = refs[2 * count :]
    role, dp, tp = places()
    roles, dps, _ = sizes()
    role_peers = [(lax.rem(role + k, roles), dp, tp) for k in range(1, roles)]
    dp_peers = [(role, lax.rem(dp + j, dps), tp) for j in range(1, dps)]
    enter(role_peers + dp_peers)
    copies = []
    for i in range(count):
        for k in range(1, roles):
            copies.append(send(ins[i], outs[i].at[dp, role], send_role.at[i, k], recv_role.at[i, k], role_peers[k - 1]))
        for j in range(1, dps):
            copies.append(send(ins[i], outs[i].at[dp, role], send_dp.at[i, j, 0], recv_dp.at[i, j, 0], dp_peers[j - 1]))
        local = pltpu.make_async_copy(ins[i], outs[i].at[dp, role], own.at[i])
        local.start()
    for i in range(count):
        for k in range(1, roles):
            slot = outs[i].at[dp, lax.rem(role + roles - k, roles)]
            landed(slot, recv_role.at[i, k])
            for j in range(1, dps):
                copies.append(send(slot, slot, send_dp.at[i, j, k], recv_dp.at[i, j, k], dp_peers[j - 1]))
    for i in range(count):
        pltpu.make_async_copy(ins[i], outs[i].at[dp, role], own.at[i]).wait()
        for j in range(1, dps):
            for k in range(roles):
                slot = outs[i].at[lax.rem(dp + dps - j, dps), lax.rem(role + roles - k, roles)]
                landed(slot, recv_dp.at[i, j, k])
    for copy in copies:
        copy.wait_send()


def gather_rows(arrays):
    roles, dps, _ = sizes()
    n = len(arrays)
    return communicate(
        functools.partial(gather_kernel, n),
        "gather_rows",
        [jax.ShapeDtypeStruct((dps, roles, *x.shape), x.dtype) for x in arrays],
        [dma(n), dma(n, roles), dma(n, roles), dma(n, dps, roles), dma(n, dps, roles)],
        0,
        arrays,
    )


def features_kernel(count, *refs):
    ins, outs = refs[:count], refs[count : 2 * count]
    slots = refs[2 * count : 3 * count]
    sends, recvs = refs[3 * count :]
    role, dp, tp = places()
    tps = sizes()[2]
    peers = [(role, dp, lax.rem(tp + k, tps)) for k in range(1, tps)]
    enter(peers)
    copies = []
    for i in range(count):
        for k in range(1, tps):
            copies.append(send(ins[i], slots[i].at[k - 1], sends.at[i, k], recvs.at[i, k], peers[k - 1]))
    for i in range(count):
        total = ins[i][...]
        for k in range(1, tps):
            landed(slots[i].at[k - 1], recvs.at[i, k])
            total = total + slots[i][k - 1]
        outs[i][...] = total
    for copy in copies:
        copy.wait_send()


def sum_features(arrays):
    tps = sizes()[2]
    n = len(arrays)
    return communicate(
        functools.partial(features_kernel, n),
        "sum_features",
        [jax.ShapeDtypeStruct(x.shape, x.dtype) for x in arrays],
        [pltpu.VMEM((max(tps - 1, 1), *x.shape), x.dtype) for x in arrays] + [dma(n, tps), dma(n, tps)],
        1,
        arrays,
    )


def tokens_kernel(count, *refs):
    ins, outs = refs[:count], refs[count : 2 * count]
    slots = refs[2 * count : 3 * count]
    sends, recvs = refs[3 * count :]
    role, dp, tp = places()
    roles, dps, _ = sizes()
    offsets = [(j, k) for k in range(roles) for j in range(dps) if (j, k) != (0, 0)]
    offsets.sort(key=lambda o: -min(o[1], roles - o[1]))
    peers = {(j, k): (lax.rem(role + k, roles), lax.rem(dp + j, dps), tp) for j, k in offsets}
    enter(list(peers.values()))
    copies = []
    for i in range(count):
        for j, k in offsets:
            peer = peers[j, k]
            copies.append(send(ins[i].at[peer[1], peer[0]], slots[i].at[j, k], sends.at[i, j, k], recvs.at[i, j, k], peer))
    for i in range(count):
        total = ins[i][dp, role].astype(jnp.float32)
        for j, k in reversed(offsets):
            landed(slots[i].at[j, k], recvs.at[i, j, k])
            total = total + slots[i][j, k].astype(jnp.float32)
        outs[i][...] = total
    for copy in copies:
        copy.wait_send()


def sum_tokens(arrays):
    roles, dps, _ = sizes()
    n = len(arrays)
    return communicate(
        functools.partial(tokens_kernel, n),
        "sum_tokens",
        [jax.ShapeDtypeStruct(x.shape[2:], jnp.float32) for x in arrays],
        [pltpu.VMEM(x.shape, x.dtype) for x in arrays] + [dma(n, dps, roles), dma(n, dps, roles)],
        2,
        arrays,
    )


def spread_kernel(a_ref, b_ref, whole_ref, slice_ref, own, send_b, recv_b, send_role, recv_role, send_dp, recv_dp, send_hi, recv_hi, send_lo, recv_lo):
    role, dp, tp = places()
    roles, dps, tps = sizes()
    half = tps // 2
    devices = roles * dps * tps
    me = (role * dps + dp) * tps + tp

    barrier = pltpu.get_barrier_semaphore()

    @pl.loop(1, devices)
    def _(step):
        other = lax.rem(me + step, devices)
        peer = (other // (dps * tps), lax.rem(other // tps, dps), lax.rem(other, tps))
        pl.semaphore_signal(barrier, inc=1, device_id=peer, device_id_type=MESH)

    pl.semaphore_wait(barrier, devices - 1)

    role_peers = [(lax.rem(role + k, roles), dp, tp) for k in range(1, roles)]
    dp_peers = [(role, lax.rem(dp + j, dps), tp) for j in range(1, dps)]
    hi_peers = [(role, dp, lax.rem(tp + 2 * h, tps)) for h in range(1, half)]
    lo_peer = (role, dp, tp + 1 - 2 * lax.rem(tp, 2))

    home = whole_ref.at[tp, dp, role]
    copies = []
    for k in range(1, roles):
        copies.append(send(a_ref, home, send_role.at[k], recv_role.at[k], role_peers[k - 1]))
    for j in range(1, dps):
        copies.append(send(a_ref, home, send_dp.at[j, 0], recv_dp.at[j, 0], dp_peers[j - 1]))
    local = pltpu.make_async_copy(a_ref, home, own.at[0])
    local.start()

    def b_copy(i, k):
        block = tp * dps + i
        peer = (lax.rem(role + k, roles), block // tps, lax.rem(block, tps))
        place = slice_ref.at[dp, role]
        remote = pltpu.make_async_remote_copy(
            src_ref=b_ref.at[i], dst_ref=place, send_sem=send_b.at[i, k], recv_sem=recv_b.at[dp, role],
            device_id=peer, device_id_type=MESH,
        )
        if k > 0:
            return None, remote, None
        here = (block // tps == dp) & (lax.rem(block, tps) == tp)
        return here, remote, pltpu.make_async_copy(b_ref.at[i], place, recv_b.at[dp, role])

    for k in range(roles):
        for i in range(dps):
            here, remote, beside = b_copy(i, k)
            if here is None:
                remote.start()
            else:
                pl.when(here)(beside.start)
                pl.when(jnp.logical_not(here))(remote.start)

    for k in range(1, roles):
        slot = whole_ref.at[tp, dp, lax.rem(role + roles - k, roles)]
        landed(slot, recv_role.at[k])
        for j in range(1, dps):
            copies.append(send(slot, slot, send_dp.at[j, k], recv_dp.at[j, k], dp_peers[j - 1]))
    local.wait()
    for j in range(dps):
        from_dp = lax.rem(dp + dps - j, dps)
        if j > 0:
            for k in range(roles):
                landed(whole_ref.at[tp, from_dp, lax.rem(role + roles - k, roles)], recv_dp.at[j, k])
        group = whole_ref.at[tp, from_dp]
        for h in range(1, half):
            copies.append(send(group, group, send_hi.at[h, j], recv_hi.at[h, j], hi_peers[h - 1]))
        copies.append(send(group, group, send_lo.at[0, j], recv_lo.at[0, j], lo_peer))
    for j in range(dps):
        from_dp = lax.rem(dp + dps - j, dps)
        for h in range(1, half):
            group = whole_ref.at[lax.rem(tp + tps - 2 * h, tps), from_dp]
            landed(group, recv_hi.at[h, j])
            copies.append(send(group, group, send_lo.at[h, j], recv_lo.at[h, j], lo_peer))
    other = lo_peer[2]
    for j in range(dps):
        from_dp = lax.rem(dp + dps - j, dps)
        for h in range(half):
            landed(whole_ref.at[lax.rem(other + tps - 2 * h, tps), from_dp], recv_lo.at[h, j])
    for d in range(dps):
        for r in range(roles):
            landed(slice_ref.at[d, r], recv_b.at[d, r])
    for k in range(roles):
        for i in range(dps):
            here, remote, _ = b_copy(i, k)
            if here is None:
                remote.wait_send()
            else:
                pl.when(jnp.logical_not(here))(remote.wait_send)
    for copy in copies:
        copy.wait_send()


def spread(a, b):
    roles, dps, tps = sizes()
    half = max(tps // 2, 1)
    return communicate(
        spread_kernel,
        "spread",
        [
            jax.ShapeDtypeStruct((tps, dps, roles, *a.shape), a.dtype),
            jax.ShapeDtypeStruct((dps, roles, *b.shape[1:]), b.dtype),
        ],
        [
            dma(1), dma(dps, roles), dma(dps, roles), dma(roles), dma(roles),
            dma(dps, roles), dma(dps, roles), dma(half, dps), dma(half, dps), dma(half, dps), dma(half, dps),
        ],
        3,
        [a, b],
    )


def merge_kernel(base_ref, b_ref, a_ref, prompts_ref, merged_ref, projected_ref):
    shards, _, width = a_ref.shape
    total = jnp.zeros(projected_ref.shape, jnp.float32)
    for shard in range(shards):
        columns = pl.ds(shard * width, width)
        delta = jnp.dot(b_ref[...], a_ref[shard], preferred_element_type=jnp.float32)
        merged = (base_ref[:, columns].astype(jnp.float32) + adapter_scale * delta).astype(jnp.bfloat16)
        merged_ref[:, columns] = merged
        total = total + contract_cols(merged, prompts_ref[:, columns])
    projected_ref[...] = total.astype(projected_ref.dtype)


def merge(base, b, a, prompts):
    rows, width = base.shape
    tile = max(t for t in range(16, 257, 16) if rows % t == 0)
    count = prompts.shape[0]
    return pl.pallas_call(
        merge_kernel,
        name="merge",
        grid=(rows // tile,),
        out_shape=[
            jax.ShapeDtypeStruct(base.shape, base.dtype),
            jax.ShapeDtypeStruct((rows, count), jnp.bfloat16),
        ],
        in_specs=[
            pl.BlockSpec((tile, width), lambda i: (i, 0)),
            pl.BlockSpec((tile, b.shape[1]), lambda i: (i, 0)),
            VMEM,
            VMEM,
        ],
        out_specs=[
            pl.BlockSpec((tile, width), lambda i: (i, 0)),
            pl.BlockSpec((tile, count), lambda i: (i, 0)),
        ],
        compiler_params=pltpu.CompilerParams(vmem_limit_bytes=56 * 1024 * 1024),
        cost_estimate=pl.CostEstimate(
            flops=2 * rows * width * (count + b.shape[1]), bytes_accessed=4 * rows * width, transcendentals=0
        ),
    )(base, b, a, prompts)


def body(
    activations,
    cotangent,
    block_keep,
    input_factor,
    input_mean,
    input_square,
    output_factor,
    output_mean,
    output_square,
    frozen_base_rows,
    prompts,
):
    roles, dps, tps = sizes()
    rows = input_factor.shape[0]
    rank = roles * dps * rows
    group_prompts = lax.all_gather(prompts, ("dp", "tp"), axis=0, tiled=True)
    input_rows, output_rows = gather_rows(
        [input_factor.astype(jnp.bfloat16), output_factor.astype(jnp.bfloat16)]
    )
    low_input = contract_cols(activations, input_rows.reshape(rank, -1))
    low_grad = contract_cols(cotangent, output_rows.reshape(rank, -1))
    low_input, low_grad = sum_features([low_input, low_grad])
    input_kept = masked(low_input, block_keep)
    grad_kept = masked(low_grad, block_keep)
    input_part = contract_rows(grad_kept, activations).astype(jnp.bfloat16)
    output_part = contract_rows(input_kept, cotangent).astype(jnp.bfloat16)
    input_sum, output_sum = sum_tokens(
        [part.reshape(dps, roles, rows, -1) for part in (input_part, output_part)]
    )
    adapter_factor_scale = adapter_scale / ROLLOUT_TOKENS
    input_new, input_moment, input_second = adam_update(
        input_factor, input_mean, input_square, input_sum * adapter_factor_scale
    )
    output_new, output_moment, output_second = adam_update(
        output_factor, output_mean, output_square, output_sum * adapter_factor_scale
    )
    input_send = input_new.astype(jnp.bfloat16)
    output_send = output_new.astype(jnp.bfloat16).reshape(rows, dps, -1).swapaxes(0, 1)
    input_whole, output_slice = spread(input_send, output_send)
    merged_weight_rows, projected = merge(
        frozen_base_rows,
        output_slice.reshape(rank, -1).T,
        input_whole.reshape(tps, rank, -1),
        group_prompts,
    )
    return (
        input_new,
        output_new,
        input_moment,
        output_moment,
        input_second,
        output_second,
        merged_weight_rows,
        projected,
    )


def solution(mesh):
    placed = (
        P(("role", "dp"), "tp"),
        P(("role", "dp"), "tp"),
        P(("role", "dp")),
        P(("role", "dp"), "tp"),
        P(("role", "dp"), "tp"),
        P(("role", "dp"), "tp"),
        P(("role", "dp"), "tp"),
        P(("role", "dp"), "tp"),
        P(("role", "dp"), "tp"),
        P(("dp", "tp"), None),
        P(("role", "dp", "tp"), None),
    )
    return jax.shard_map(
        body,
        mesh=mesh,
        in_specs=placed,
        out_specs=(
            P(("role", "dp"), "tp"),
            P(("role", "dp"), "tp"),
            P(("role", "dp"), "tp"),
            P(("role", "dp"), "tp"),
            P(("role", "dp"), "tp"),
            P(("role", "dp"), "tp"),
            P(("dp", "tp"), None),
            P(("dp", "tp"), "role"),
        ),
        check_vma=False,
    )
```

time: 324 us -> 134 us (0.41)
  blocking collectives: 130 us -> 0 us
  waiting for transfers between devices: 127 us -> 0.68 us
  Pallas kernels: 0 us -> 110 us
  matrix products: 47.2 us -> 1.84 us
    all_gather x4 -> x0, blocking collectives: 130 us -> none  [the longest x1 33.1 us: body(): lax.all_gather(output_send, ('role', 'dp'), axis=0, tiled=True)]
    pallas_call x0 -> x5, Pallas kernels: none -> 110 us  [the longest x4 81.6 us: communicate(): pl.pallas_call(kernel, name=name, out_shape=outs, in_specs=[VMEM] * len(a...]
    reduce_scatter x4 -> x0, waiting for transfers between devices: 57.8 us -> none  [the longest x1 26.3 us: body(): lax.psum_scatter(output_part, 'role', scatter_dimension=0, tiled=True)]
    psum x1 -> x0, waiting for transfers between devices: 32.8 us -> none  [body(): low_input, low_grad = lax.psum((low_input, low_grad), 'tp')]
    dot_general x3 -> x2, matrix products: 28.1 us -> 0.79 us  [contract_rows(): lax.dot_general(left, right, (((0,), (0,)), ((), ())), preferred_element_...]
    all_gather x2 -> x0, waiting for transfers between devices: 20.4 us -> none  [the longest x1 20.4 us: body(): lax.all_gather(output_cols, 'tp', axis=1, tiled=True)]
    all_gather x1, waiting for transfers between devices: 14.7 us -> 0.01 us  [body(): group_prompts = lax.all_gather(prompts, ('dp', 'tp'), axis=0, tiled=True)]
    dot_general x1 -> x2, matrix products: 15.4 us -> 1.05 us  [contract_cols(): lax.dot_general(left, right, (((1,), (1,)), ((), ())), preferred_element_...]
  transfers between devices with their start and end apart: 8 -> 1, of which waited for: 6 -> 0; matrix products, arithmetic and copies ran while one was open for 9% -> 5% of each run, Pallas kernels for 0% -> 61%
where the time goes in v1:
time: 134 us; the launch traced here: 133 us
  Pallas kernels  110 us (82%)
  between operations  14.8 us (11%)
  other arithmetic  3.21 us (2%)
  local copies, waits for them, and re-layouts  2.03 us (2%)
  matrix products  1.84 us (1%)
    pallas_call x4, Pallas kernels, communicate(): pl.pallas_call(kernel, name=name, out_shape=outs, in_specs=[VMEM] * len(a...  81.6 us
    pallas_call x1, Pallas kernels, merge(): pl.pallas_call(merge_kernel, name='merge', grid=(rows // tile,), out_shap...  28.5 us
  transfers between devices with their start and end apart: 1, of which 0 were waited for; matrix products, arithmetic and copies ran while one was open for 5% of the time, Pallas kernels for 61%

profile of v1, /device:TPU:0, one launch (start us, length us, event | category | flops | bytes accessed | tf_op | source)
XLA Modules:
  0.0 132.7 jit_solution(15018102060724141182)
XLA Ops:
  7.2 0.0 copy-start
  7.2 0.0 all-gather.2.cloned.1.call-start
  7.2 0.7 all-gather.2.cloned.1.call-update
  8.6 0.8 convert_element_type.28.refs_0_
  9.4 0.9 convert_element_type.29.refs_1_
  10.3 0.0 copy-start.3
  10.3 22.2 %gather_rows.1 = (bf16[2,4,8,2048]{3,2,1,0:T(8,128)(2,1)S(1)}, bf16[2,4,8,3584]{3,2,1,0:T(8,128)(2,1)S(1)}) custom-call(bf16[8,2048]{1,0:T(8,128)(2,1)S(1)} %convert_element_type.28.refs_0_, bf16[8,3584]{1,0:T(8,128)(2,1)S(1)} %convert_element_type.29.refs_1_), custom_call_target="tpu_custom_call" | custom-call | flops 1000000000 | bytes 10000000 | tf_op jit(solution)/shard_map/gather_rows/pallas_call | solution.py:87
  32.5 0.0 copy-done.3
  32.5 0.4 convolution_bitcast_fusion.1.refs_0_
  33.0 0.0 copy-done
  33.0 0.6 convolution_bitcast_fusion.refs_1_
  33.6 23.2 %sum_features.1 = (f32[256,64]{1,0:T(8,128)S(1)}, f32[256,64]{1,0:T(8,128)S(1)}) custom-call(f32[256,64]{1,0:T(8,128)S(1)} %convolution_bitcast_fusion.1.refs_0_, f32[256,64]{1,0:T(8,128)S(1)} %convolution_bitcast_fusion.refs_1_), custom_call_target="tpu_custom_call" | custom-call | flops 1000000000 | bytes 10000000 | tf_op jit(solution)/shard_map/sum_features/pallas_call | solution.py:87
  56.8 0.3 convolution_convert_fusion.1
  57.2 0.5 convolution_convert_fusion
  57.6 0.0 copy-start.5
  57.6 0.0 copy-start.8
  57.6 0.0 copy-start.9
  57.7 0.0 copy-start.4
  57.7 0.0 copy-start.6
  57.7 0.0 copy-start.7
  57.7 18.8 %sum_tokens.1 = (f32[8,2048]{1,0:T(8,128)S(1)}, f32[8,3584]{1,0:T(8,128)S(1)}) custom-call(bf16[2,4,8,2048]{3,2,1,0:T(8,128)(2,1)S(1)} %bitcast.24, bf16[2,4,8,3584]{3,2,1,0:T(8,128)(2,1)S(1)} %bitcast.23), custom_call_target="tpu_custom_call" | custom-call | flops 1000000000 | bytes 10000000 | tf_op jit(solution)/shard_map/sum_tokens/pallas_call | solution.py:87
  76.5 0.0 copy-done.5
  76.5 0.0 copy-done.8
  76.5 0.0 copy-done.9
  76.6 0.7 fusion.3
  77.3 0.0 copy-done.4
  77.3 0.0 copy-done.6
  77.3 0.0 copy-done.7
  77.3 0.8 fusion.2
  78.0 17.3 %spread.1 = (bf16[4,2,4,8,2048]{4,3,2,1,0:T(8,128)(2,1)S(1)}, bf16[2,4,8,1792]{3,2,1,0:T(8,128)(2,1)S(1)}) custom-call(bf16[8,2048]{1,0:T(8,128)(2,1)S(1)} %get-tuple-element.32.a_ref, bf16[2,8,1792]{2,1,0:T(8,128)(2,1)S(1)} %bitcast.27), custom_call_target="tpu_custom_call" | custom-call | flops 1000000000 | bytes 10000000 | tf_op jit(solution)/shard_map/spread/pallas_call | solution.py:87
  95.4 0.0 copy-start.2
  95.4 1.0 copy-done.2
  96.3 1.0 copy.24
  97.3 0.0 all-gather.2.cloned.1.call-done.prompts_ref
  97.3 0.0 copy-start.1
  97.3 28.5 %merge.1 = (bf16[1792,8192]{1,0:T(8,128)(2,1)}, bf16[1792,256]{1,0:T(8,128)(2,1)}) custom-call(bf16[1792,8192]{1,0:T(8,128)(2,1)} %base_ref.1, bf16[1792,64]{1,0:T(8,128)(2,1)} %bitcast.28, bf16[4,64,2048]{2,1,0:T(8,128)(2,1)} %bitcast.21, bf16[256,8192]{1,0:T(8,128)(2,1)} %all-gather.2.cloned.1.call-done.prompts_ref), custom_call_target="tpu_custom_call" | custom-call | flops 9395240960 | bytes 58720256 | tf_op jit(solution)/shard_map/merge/pallas_call | solution.py:355
  125.8 0.0 copy-done.1
Async XLA Ops:
  7.2 25.8 %copy-start = (bf16[256,3584]{1,0:T(8,128)(2,1)S(1)}, bf16[256,3584]{1,0:T(8,128)(2,1)}, u32[]{:S(2)}) copy-start(bf16[256,3584]{1,0:T(8,128)(2,1)} %param.12) | copy-start | bytes 5505028
  7.2 90.2 %all-gather.2.cloned.1.call-start = ((), (), s32[]{:S(2)}) async-start(), calls=%async_computation | async-start | bytes 4718592 | tf_op jit(solution)/shard_map/all_gather | solution.py:396
  10.3 22.2 %copy-start.3 = (bf16[256,2048]{1,0:T(8,128)(2,1)S(1)}, bf16[256,2048]{1,0:T(8,128)(2,1)}, u32[]{:S(2)}) copy-start(bf16[256,2048]{1,0:T(8,128)(2,1)} %param.11) | copy-start | bytes 3145732
  57.6 18.9 %copy-start.5 = (f32[8,2048]{1,0:T(8,128)S(1)}, f32[8,2048]{1,0:T(8,128)}, u32[]{:S(2)}) copy-start(f32[8,2048]{1,0:T(8,128)} %param.14) | copy-start | bytes 196612
  57.6 18.9 %copy-start.8 = (f32[8,2048]{1,0:T(8,128)S(1)}, f32[8,2048]{1,0:T(8,128)}, u32[]{:S(2)}) copy-start(f32[8,2048]{1,0:T(8,128)} %param.15) | copy-start | bytes 196612
  57.6 18.9 %copy-start.9 = (f32[8,2048]{1,0:T(8,128)S(1)}, f32[8,2048]{1,0:T(8,128)}, u32[]{:S(2)}) copy-start(f32[8,2048]{1,0:T(8,128)} %param.16) | copy-start | bytes 196612
  57.7 19.6 %copy-start.4 = (f32[8,3584]{1,0:T(8,128)S(1)}, f32[8,3584]{1,0:T(8,128)}, u32[]{:S(2)}) copy-start(f32[8,3584]{1,0:T(8,128)} %param.17) | copy-start | bytes 344068
  57.7 19.6 %copy-start.6 = (f32[8,3584]{1,0:T(8,128)S(1)}, f32[8,3584]{1,0:T(8,128)}, u32[]{:S(2)}) copy-start(f32[8,3584]{1,0:T(8,128)} %param.18) | copy-start | bytes 344068
  57.7 19.6 %copy-start.7 = (f32[8,3584]{1,0:T(8,128)S(1)}, f32[8,3584]{1,0:T(8,128)}, u32[]{:S(2)}) copy-start(f32[8,3584]{1,0:T(8,128)} %param.19) | copy-start | bytes 344068
  95.4 1.0 copy-start.2
  97.3 28.5 %copy-start.1 = (bf16[256,3584]{1,0:T(8,128)(2,1)S(1)}, bf16[256,3584]{1,0:T(8,128)(2,1)}, u32[]{:S(2)}) copy-start(bf16[256,3584]{1,0:T(8,128)(2,1)} %param.12) | copy-start | bytes 5505028
Sparse Core Ops, SparseCore 0:
  9.9 50.8 all-gather.1
